TPU v7x, 32 devices: a whole 2x2x4 slice. The times are simulated.
32 devices in a mesh: wide: 8 (over z, core), narrow: 4 (over y, x).
Axes of the slice: x: 2, y: 2, z: 4, core: 2. Of those that a mesh axis runs over, the one named last changes fastest.
Arguments:
- operator: bfloat16 [8, 4, 2, 2048, 2048], P('wide', 'narrow'), may hold values from -0.125 to 0.125
- sources: bfloat16 [8, 4, 2048, 128], P('wide', 'narrow'), may hold values from -6 to 6
- face_lengths: int32 [8, 4, 4], P('wide', 'narrow'), may hold values from 192 to 640, as said below
Outputs:
- outgoing: bfloat16 [8, 4, 2048, 128], P('wide', 'narrow')
- incoming: bfloat16 [8, 4, 2048, 128], P('wide', 'narrow')
Inputs may be any that keep to these rules, and one draw needn't show every extreme that they name: `face_lengths`: the entries of adjacent subdomains for their common face are equal; lower-row and higher-row entries lie in 320 to 640, column entries in 192 to 384.
All inputs are finite; a program needn't handle non-finite values.
Results may differ from a plain program's by a relative error of at most 0.0055.
Values may be sent and summed in bfloat16 or wider, within the bound.
A program may use at most 64 MiB of HBM per device.

v0:
```python
import jax
import jax.numpy as jnp
from jax import lax
from jax.sharding import PartitionSpec as P

FACE_LONG = 640
FACE_SHORT = 384
ITERS = 3


def shifted(value, axis, steps):
    count = lax.axis_size(axis)
    leading, last = (max(0, -steps), min(count, count - steps))
    return lax.ppermute(value, axis, [(source, source + steps) for source in range(leading, last)])


def live_rows(counts, total):
    rows = jnp.arange(total, dtype=jnp.int32)
    edges = [0, FACE_LONG, 2 * FACE_LONG, 2 * FACE_LONG + FACE_SHORT]
    live = jnp.zeros((total,), dtype=bool)
    for face in range(4):
        live = live | (rows >= edges[face]) & (rows < edges[face] + counts[face])
    return live[:, None]


def trade(out):
    low = FACE_LONG
    mid = 2 * FACE_LONG
    high = 2 * FACE_LONG + FACE_SHORT
    from_lower = shifted(out[low:mid], "wide", 1)
    from_upper = shifted(out[:low], "wide", -1)
    from_left = shifted(out[high:], "narrow", 1)
    from_right = shifted(out[mid:high], "narrow", -1)
    return (from_lower, from_upper, from_left, from_right)


def complex_terms(first, second):
    half = first.shape[1] // 2
    real_part = first[:, :half] - second[:, half:]
    imag_part = first[:, half:] + second[:, :half]
    return jnp.concatenate([real_part, imag_part], axis=1)


def apply_operator(oper, pieces):
    first = None
    second = None
    start = 0
    for piece in pieces:
        stop = start + piece.shape[0]
        part_one = jnp.dot(oper[0, :, start:stop], piece, preferred_element_type=jnp.float32)
        part_two = jnp.dot(oper[1, :, start:stop], piece, preferred_element_type=jnp.float32)
        first = part_one if first is None else first + part_one
        second = part_two if second is None else second + part_two
        start = stop
    return complex_terms(first, second)


def body(operator, sources, face_lengths):
    oper = operator[0, 0]
    source_block = sources[0, 0]
    counts = face_lengths[0, 0]
    total = oper.shape[-1]
    live = live_rows(counts, total)
    masked = jnp.where(live, source_block, jnp.zeros_like(source_block))
    pieces = trade(masked)
    outgoing = masked
    for step in range(ITERS):
        terms = apply_operator(oper, pieces) + source_block.astype(jnp.float32)
        outgoing = jnp.where(live, terms, jnp.zeros_like(terms)).astype(jnp.bfloat16)
        pieces = trade(outgoing)
    incoming = jnp.concatenate(pieces, axis=0)
    return (outgoing[None, None], incoming[None, None])


def solution(mesh):
    in_specs = (
        P("wide", "narrow", None, None, None),
        P("wide", "narrow", None, None),
        P("wide", "narrow", None),
    )
    out_specs = (P("wide", "narrow", None, None), P("wide", "narrow", None, None))
    return jax.shard_map(body, mesh=mesh, in_specs=in_specs, out_specs=out_specs, check_vma=False)
```

profile of v0, /device:TPU:1, one launch (start us, length us, event | category | flops | bytes accessed | tf_op | source)
XLA Modules:
  0.0 87.6 jit_solution(820910909549614151)
XLA Ops:
  0.6 1.5 %fusion.58 = (s32[1,1,1]{2,1,0:T(1,128)}, s32[1,1,1]{2,1,0:T(1,128)}, s32[1,1,1]{2,1,0:T(1,128)}, s32[1,1,1]{2,1,0:T(1,128)}) fusion(s32[1,1,4]{2,1,0:T(1,128)} %param.5), kind=kLoop, calls=%fused_computation.91 | loop fusion | bytes 32 | tf_op jit(solution)/shard_map/slice | solution.py:22
  2.1 1.2 %copy.5 = bf16[1,1,2048,128]{2,3,1,0:T(8,128)(2,1)S(1)} copy(bf16[1,1,2048,128]{3,2,1,0:T(8,128)(2,1)} %param.4) | data formatting | bytes 1048576 | tf_op args[1]
  6.9 4.2 %collective-permute-start.2 = (bf16[384,128]{0,1:T(8,128)(2,1)S(1)}, bf16[384,128]{0,1:T(8,128)(2,1)S(1)}, u32[]{:S(2)}, u32[]{:S(2)}) collective-permute-start(bf16[384,128]{0,1:T(8,128)(2,1)S(1)} %get-tuple-element.24), channel_id=1, source_target_pairs={{0,1},{1,2},{2,3},{4,5},{5,6},{6,7},{8,9},{9,10},{10,11},{12,13},{... | collective-permute-start | bytes 294920 | tf_op jit(solution)/shard_map/ppermute | solution.py:14
  11.1 2.9 %collective-permute-start.1 = (bf16[640,128]{0,1:T(8,128)(2,1)S(1)}, bf16[640,128]{0,1:T(8,128)(2,1)S(1)}, u32[]{:S(2)}, u32[]{:S(2)}) collective-permute-start(bf16[640,128]{0,1:T(8,128)(2,1)S(1)} %get-tuple-element.23), channel_id=1, source_target_pairs={{4,0},{8,4},{12,8},{16,12},{20,16},{24,20},{28,24},{5,1},{9,5},{13... | collective-permute-start | bytes 491528 | tf_op jit(solution)/shard_map/ppermute | solution.py:14
  14.0 1.3 %collective-permute-start.3 = (bf16[384,128]{0,1:T(8,128)(2,1)S(1)}, bf16[384,128]{0,1:T(8,128)(2,1)S(1)}, u32[]{:S(2)}, u32[]{:S(2)}) collective-permute-start(bf16[384,128]{0,1:T(8,128)(2,1)S(1)} %get-tuple-element.25), channel_id=1, source_target_pairs={{1,0},{2,1},{3,2},{5,4},{6,5},{7,6},{9,8},{10,9},{11,10},{13,12},{... | collective-permute-start | bytes 294920 | tf_op jit(solution)/shard_map/ppermute | solution.py:14
  15.3 3.1 %collective-permute-start = (bf16[640,128]{0,1:T(8,128)(2,1)S(1)}, bf16[640,128]{0,1:T(8,128)(2,1)S(1)}, u32[]{:S(2)}, u32[]{:S(2)}) collective-permute-start(bf16[640,128]{0,1:T(8,128)(2,1)S(1)} %get-tuple-element.22), channel_id=1, source_target_pairs={{0,4},{4,8},{8,12},{12,16},{16,20},{20,24},{24,28},{1,5},{5,9},{9,... | collective-permute-start | bytes 491528 | tf_op jit(solution)/shard_map/ppermute | solution.py:14
  18.4 2.0 %fusion.26 = f32[128,2048]{1,0:T(8,128)S(1)} fusion(bf16[384,128]{0,1:T(8,128)(2,1)S(1)} %collective-permute-done.2, bf16[2,2048,2048]{2,1,0:T(8,128)(2,1)} %bitcast.90), kind=kOutput, calls=%fused_computation.43 | convolution fusion | flops 201326592 | bytes 2719744 | tf_op jit(solution)/shard_map/dot_general | solution.py:50
  20.4 2.0 %fusion.32 = f32[128,2048]{1,0:T(8,128)S(1)} fusion(bf16[384,128]{0,1:T(8,128)(2,1)S(1)} %collective-permute-done.2, bf16[2,2048,2048]{2,1,0:T(8,128)(2,1)} %bitcast.91), kind=kOutput, calls=%fused_computation.49 | convolution fusion | flops 201326592 | bytes 2719744 | tf_op jit(solution)/shard_map/dot_general | solution.py:51
  22.5 2.0 %fusion.29 = f32[128,2048]{1,0:T(8,128)S(1)} fusion(bf16[384,128]{0,1:T(8,128)(2,1)S(1)} %collective-permute-done.3, bf16[2,2048,2048]{2,1,0:T(8,128)(2,1)} %bitcast.92), kind=kOutput, calls=%fused_computation.46 | convolution fusion | flops 201326592 | bytes 2719744 | tf_op jit(solution)/shard_map/dot_general | solution.py:50
  24.5 2.0 %fusion.35 = f32[128,2048]{1,0:T(8,128)S(1)} fusion(bf16[384,128]{0,1:T(8,128)(2,1)S(1)} %collective-permute-done.3, bf16[2,2048,2048]{2,1,0:T(8,128)(2,1)} %bitcast.93), kind=kOutput, calls=%fused_computation.52 | convolution fusion | flops 201326592 | bytes 2719744 | tf_op jit(solution)/shard_map/dot_general | solution.py:51
  26.6 2.7 %fusion.20 = f32[128,2048]{1,0:T(8,128)S(1)} fusion(bf16[640,128]{0,1:T(8,128)(2,1)S(1)} %collective-permute-done.1, bf16[2,2048,2048]{2,1,0:T(8,128)(2,1)} %bitcast.94), kind=kOutput, calls=%fused_computation.30 | convolution fusion | flops 335544320 | bytes 3833856 | tf_op jit(solution)/shard_map/dot_general | solution.py:50
  32.6 4.3 %collective-permute-start.6 = (bf16[384,128]{0,1:T(8,128)(2,1)S(1)}, bf16[384,128]{0,1:T(8,128)(2,1)S(1)}, u32[]{:S(2)}, u32[]{:S(2)}) collective-permute-start(bf16[384,128]{0,1:T(8,128)(2,1)S(1)} %get-tuple-element.20), channel_id=1, source_target_pairs={{0,1},{1,2},{2,3},{4,5},{5,6},{6,7},{8,9},{9,10},{10,11},{12,13},{... | collective-permute-start | bytes 294920 | tf_op jit(solution)/shard_map/ppermute | solution.py:14
  36.9 1.9 %collective-permute-start.5 = (bf16[640,128]{0,1:T(8,128)(2,1)S(1)}, bf16[640,128]{0,1:T(8,128)(2,1)S(1)}, u32[]{:S(2)}, u32[]{:S(2)}) collective-permute-start(bf16[640,128]{0,1:T(8,128)(2,1)S(1)} %get-tuple-element.19), channel_id=1, source_target_pairs={{4,0},{8,4},{12,8},{16,12},{20,16},{24,20},{28,24},{5,1},{9,5},{13... | collective-permute-start | bytes 491528 | tf_op jit(solution)/shard_map/ppermute | solution.py:14
  38.8 1.3 %collective-permute-start.7 = (bf16[384,128]{0,1:T(8,128)(2,1)S(1)}, bf16[384,128]{0,1:T(8,128)(2,1)S(1)}, u32[]{:S(2)}, u32[]{:S(2)}) collective-permute-start(bf16[384,128]{0,1:T(8,128)(2,1)S(1)} %get-tuple-element.21), channel_id=1, source_target_pairs={{1,0},{2,1},{3,2},{5,4},{6,5},{7,6},{9,8},{10,9},{11,10},{13,12},{... | collective-permute-start | bytes 294920 | tf_op jit(solution)/shard_map/ppermute | solution.py:14
  40.1 3.6 %collective-permute-start.4 = (bf16[640,128]{0,1:T(8,128)(2,1)S(1)}, bf16[640,128]{0,1:T(8,128)(2,1)S(1)}, u32[]{:S(2)}, u32[]{:S(2)}) collective-permute-start(bf16[640,128]{0,1:T(8,128)(2,1)S(1)} %get-tuple-element.18), channel_id=1, source_target_pairs={{0,4},{4,8},{8,12},{12,16},{16,20},{20,24},{24,28},{1,5},{5,9},{9,... | collective-permute-start | bytes 491528 | tf_op jit(solution)/shard_map/ppermute | solution.py:14
  50.7 4.7 %collective-permute-start.10 = (bf16[384,128]{0,1:T(8,128)(2,1)S(1)}, bf16[384,128]{0,1:T(8,128)(2,1)S(1)}, u32[]{:S(2)}, u32[]{:S(2)}) collective-permute-start(bf16[384,128]{0,1:T(8,128)(2,1)S(1)} %get-tuple-element.16), channel_id=1, source_target_pairs={{0,1},{1,2},{2,3},{4,5},{5,6},{6,7},{8,9},{9,10},{10,11},{12,13},{... | collective-permute-start | bytes 294920 | tf_op jit(solution)/shard_map/ppermute | solution.py:14
  55.4 1.9 %collective-permute-start.9 = (bf16[640,128]{0,1:T(8,128)(2,1)S(1)}, bf16[640,128]{0,1:T(8,128)(2,1)S(1)}, u32[]{:S(2)}, u32[]{:S(2)}) collective-permute-start(bf16[640,128]{0,1:T(8,128)(2,1)S(1)} %get-tuple-element.15), channel_id=1, source_target_pairs={{4,0},{8,4},{12,8},{16,12},{20,16},{24,20},{28,24},{5,1},{9,5},{13... | collective-permute-start | bytes 491528 | tf_op jit(solution)/shard_map/ppermute | solution.py:14
  57.3 1.3 %collective-permute-start.11 = (bf16[384,128]{0,1:T(8,128)(2,1)S(1)}, bf16[384,128]{0,1:T(8,128)(2,1)S(1)}, u32[]{:S(2)}, u32[]{:S(2)}) collective-permute-start(bf16[384,128]{0,1:T(8,128)(2,1)S(1)} %get-tuple-element.17), channel_id=1, source_target_pairs={{1,0},{2,1},{3,2},{5,4},{6,5},{7,6},{9,8},{10,9},{11,10},{13,12},{... | collective-permute-start | bytes 294920 | tf_op jit(solution)/shard_map/ppermute | solution.py:14
  58.6 4.7 %collective-permute-start.8 = (bf16[640,128]{0,1:T(8,128)(2,1)S(1)}, bf16[640,128]{0,1:T(8,128)(2,1)S(1)}, u32[]{:S(2)}, u32[]{:S(2)}) collective-permute-start(bf16[640,128]{0,1:T(8,128)(2,1)S(1)} %get-tuple-element.14), channel_id=1, source_target_pairs={{0,4},{4,8},{8,12},{12,16},{16,20},{20,24},{24,28},{1,5},{5,9},{9,... | collective-permute-start | bytes 491528 | tf_op jit(solution)/shard_map/ppermute | solution.py:14
  70.2 4.3 %collective-permute-start.12 = (bf16[640,128]{0,1:T(8,128)(2,1)S(1)}, bf16[640,128]{0,1:T(8,128)(2,1)S(1)}, u32[]{:S(2)}, u32[]{:S(2)}) collective-permute-start(bf16[640,128]{0,1:T(8,128)(2,1)S(1)} %get-tuple-element.10), channel_id=1, source_target_pairs={{0,4},{4,8},{8,12},{12,16},{16,20},{20,24},{24,28},{1,5},{5,9},{9,... | collective-permute-start | bytes 491528 | tf_op jit(solution)/shard_map/ppermute | solution.py:14
  74.5 1.9 %collective-permute-start.13 = (bf16[640,128]{0,1:T(8,128)(2,1)S(1)}, bf16[640,128]{0,1:T(8,128)(2,1)S(1)}, u32[]{:S(2)}, u32[]{:S(2)}) collective-permute-start(bf16[640,128]{0,1:T(8,128)(2,1)S(1)} %get-tuple-element.11), channel_id=1, source_target_pairs={{4,0},{8,4},{12,8},{16,12},{20,16},{24,20},{28,24},{5,1},{9,5},{13... | collective-permute-start | bytes 491528 | tf_op jit(solution)/shard_map/ppermute | solution.py:14
  76.4 4.0 %collective-permute-start.14 = (bf16[384,128]{0,1:T(8,128)(2,1)S(1)}, bf16[384,128]{0,1:T(8,128)(2,1)S(1)}, u32[]{:S(2)}, u32[]{:S(2)}) collective-permute-start(bf16[384,128]{0,1:T(8,128)(2,1)S(1)} %get-tuple-element.12), channel_id=1, source_target_pairs={{0,1},{1,2},{2,3},{4,5},{5,6},{6,7},{8,9},{9,10},{10,11},{12,13},{... | collective-permute-start | bytes 294920 | tf_op jit(solution)/shard_map/ppermute | solution.py:14
  80.5 1.3 %collective-permute-start.15 = (bf16[384,128]{0,1:T(8,128)(2,1)S(1)}, bf16[384,128]{0,1:T(8,128)(2,1)S(1)}, u32[]{:S(2)}, u32[]{:S(2)}) collective-permute-start(bf16[384,128]{0,1:T(8,128)(2,1)S(1)} %get-tuple-element.13), channel_id=1, source_target_pairs={{1,0},{2,1},{3,2},{5,4},{6,5},{7,6},{9,8},{10,9},{11,10},{13,12},{... | collective-permute-start | bytes 294920 | tf_op jit(solution)/shard_map/ppermute | solution.py:14
  83.0 3.5 %collective-permute-done.15 = bf16[384,128]{0,1:T(8,128)(2,1)S(1)} collective-permute-done((bf16[384,128]{0,1:T(8,128)(2,1)S(1)}, bf16[384,128]{0,1:T(8,128)(2,1)S(1)}, u32[]{:S(2)}, u32[]{:S(2)}) %collective-permute-start.15) | collective-permute-done | bytes 98336 | tf_op jit(solution)/shard_map/ppermute | solution.py:14
  (56 shorter events, 20.2 us)
Async XLA Ops:
  3.4 25.9 %copy-start = (bf16[1,1,2,2048,2048]{4,3,2,1,0:T(8,128)(2,1)S(1)}, bf16[1,1,2,2048,2048]{4,3,2,1,0:T(8,128)(2,1)}, u32[]{:S(2)}) copy-start(bf16[1,1,2,2048,2048]{4,3,2,1,0:T(8,128)(2,1)} %param.3) | copy-start | bytes 50331652
  6.9 11.5 %collective-permute-start.2 = (bf16[384,128]{0,1:T(8,128)(2,1)S(1)}, bf16[384,128]{0,1:T(8,128)(2,1)S(1)}, u32[]{:S(2)}, u32[]{:S(2)}) collective-permute-start(bf16[384,128]{0,1:T(8,128)(2,1)S(1)} %get-tuple-element.24), channel_id=1, source_target_pairs={{0,1},{1,2},{2,3},{4,5},{5,6},{6,7},{8,9},{9,10},{10,11},{12,13},{... | collective-permute-start | bytes 294920 | tf_op jit(solution)/shard_map/ppermute | solution.py:14
  11.1 15.4 %collective-permute-start.1 = (bf16[640,128]{0,1:T(8,128)(2,1)S(1)}, bf16[640,128]{0,1:T(8,128)(2,1)S(1)}, u32[]{:S(2)}, u32[]{:S(2)}) collective-permute-start(bf16[640,128]{0,1:T(8,128)(2,1)S(1)} %get-tuple-element.23), channel_id=1, source_target_pairs={{4,0},{8,4},{12,8},{16,12},{20,16},{24,20},{28,24},{5,1},{9,5},{13... | collective-permute-start | bytes 491528 | tf_op jit(solution)/shard_map/ppermute | solution.py:14
  14.0 8.5 %collective-permute-start.3 = (bf16[384,128]{0,1:T(8,128)(2,1)S(1)}, bf16[384,128]{0,1:T(8,128)(2,1)S(1)}, u32[]{:S(2)}, u32[]{:S(2)}) collective-permute-start(bf16[384,128]{0,1:T(8,128)(2,1)S(1)} %get-tuple-element.25), channel_id=1, source_target_pairs={{1,0},{2,1},{3,2},{5,4},{6,5},{7,6},{9,8},{10,9},{11,10},{13,12},{... | collective-permute-start | bytes 294920 | tf_op jit(solution)/shard_map/ppermute | solution.py:14
  15.3 15.0 %collective-permute-start = (bf16[640,128]{0,1:T(8,128)(2,1)S(1)}, bf16[640,128]{0,1:T(8,128)(2,1)S(1)}, u32[]{:S(2)}, u32[]{:S(2)}) collective-permute-start(bf16[640,128]{0,1:T(8,128)(2,1)S(1)} %get-tuple-element.22), channel_id=1, source_target_pairs={{0,4},{4,8},{8,12},{12,16},{16,20},{20,24},{24,28},{1,5},{5,9},{9,... | collective-permute-start | bytes 491528 | tf_op jit(solution)/shard_map/ppermute | solution.py:14
  32.6 11.2 %collective-permute-start.6 = (bf16[384,128]{0,1:T(8,128)(2,1)S(1)}, bf16[384,128]{0,1:T(8,128)(2,1)S(1)}, u32[]{:S(2)}, u32[]{:S(2)}) collective-permute-start(bf16[384,128]{0,1:T(8,128)(2,1)S(1)} %get-tuple-element.20), channel_id=1, source_target_pairs={{0,1},{1,2},{2,3},{4,5},{5,6},{6,7},{8,9},{9,10},{10,11},{12,13},{... | collective-permute-start | bytes 294920 | tf_op jit(solution)/shard_map/ppermute | solution.py:14
  36.9 9.5 %collective-permute-start.5 = (bf16[640,128]{0,1:T(8,128)(2,1)S(1)}, bf16[640,128]{0,1:T(8,128)(2,1)S(1)}, u32[]{:S(2)}, u32[]{:S(2)}) collective-permute-start(bf16[640,128]{0,1:T(8,128)(2,1)S(1)} %get-tuple-element.19), channel_id=1, source_target_pairs={{4,0},{8,4},{12,8},{16,12},{20,16},{24,20},{28,24},{5,1},{9,5},{13... | collective-permute-start | bytes 491528 | tf_op jit(solution)/shard_map/ppermute | solution.py:14
  38.8 6.2 %collective-permute-start.7 = (bf16[384,128]{0,1:T(8,128)(2,1)S(1)}, bf16[384,128]{0,1:T(8,128)(2,1)S(1)}, u32[]{:S(2)}, u32[]{:S(2)}) collective-permute-start(bf16[384,128]{0,1:T(8,128)(2,1)S(1)} %get-tuple-element.21), channel_id=1, source_target_pairs={{1,0},{2,1},{3,2},{5,4},{6,5},{7,6},{9,8},{10,9},{11,10},{13,12},{... | collective-permute-start | bytes 294920 | tf_op jit(solution)/shard_map/ppermute | solution.py:14
  40.1 8.2 %collective-permute-start.4 = (bf16[640,128]{0,1:T(8,128)(2,1)S(1)}, bf16[640,128]{0,1:T(8,128)(2,1)S(1)}, u32[]{:S(2)}, u32[]{:S(2)}) collective-permute-start(bf16[640,128]{0,1:T(8,128)(2,1)S(1)} %get-tuple-element.18), channel_id=1, source_target_pairs={{0,4},{4,8},{8,12},{12,16},{16,20},{20,24},{24,28},{1,5},{5,9},{9,... | collective-permute-start | bytes 491528 | tf_op jit(solution)/shard_map/ppermute | solution.py:14
  50.7 12.6 %collective-permute-start.10 = (bf16[384,128]{0,1:T(8,128)(2,1)S(1)}, bf16[384,128]{0,1:T(8,128)(2,1)S(1)}, u32[]{:S(2)}, u32[]{:S(2)}) collective-permute-start(bf16[384,128]{0,1:T(8,128)(2,1)S(1)} %get-tuple-element.16), channel_id=1, source_target_pairs={{0,1},{1,2},{2,3},{4,5},{5,6},{6,7},{8,9},{9,10},{10,11},{12,13},{... | collective-permute-start | bytes 294920 | tf_op jit(solution)/shard_map/ppermute | solution.py:14
  55.4 10.5 %collective-permute-start.9 = (bf16[640,128]{0,1:T(8,128)(2,1)S(1)}, bf16[640,128]{0,1:T(8,128)(2,1)S(1)}, u32[]{:S(2)}, u32[]{:S(2)}) collective-permute-start(bf16[640,128]{0,1:T(8,128)(2,1)S(1)} %get-tuple-element.15), channel_id=1, source_target_pairs={{4,0},{8,4},{12,8},{16,12},{20,16},{24,20},{28,24},{5,1},{9,5},{13... | collective-permute-start | bytes 491528 | tf_op jit(solution)/shard_map/ppermute | solution.py:14
  57.3 7.2 %collective-permute-start.11 = (bf16[384,128]{0,1:T(8,128)(2,1)S(1)}, bf16[384,128]{0,1:T(8,128)(2,1)S(1)}, u32[]{:S(2)}, u32[]{:S(2)}) collective-permute-start(bf16[384,128]{0,1:T(8,128)(2,1)S(1)} %get-tuple-element.17), channel_id=1, source_target_pairs={{1,0},{2,1},{3,2},{5,4},{6,5},{7,6},{9,8},{10,9},{11,10},{13,12},{... | collective-permute-start | bytes 294920 | tf_op jit(solution)/shard_map/ppermute | solution.py:14
  58.6 9.2 %collective-permute-start.8 = (bf16[640,128]{0,1:T(8,128)(2,1)S(1)}, bf16[640,128]{0,1:T(8,128)(2,1)S(1)}, u32[]{:S(2)}, u32[]{:S(2)}) collective-permute-start(bf16[640,128]{0,1:T(8,128)(2,1)S(1)} %get-tuple-element.14), channel_id=1, source_target_pairs={{0,4},{4,8},{8,12},{12,16},{16,20},{20,24},{24,28},{1,5},{5,9},{9,... | collective-permute-start | bytes 491528 | tf_op jit(solution)/shard_map/ppermute | solution.py:14
  70.2 16.3 %collective-permute-start.12 = (bf16[640,128]{0,1:T(8,128)(2,1)S(1)}, bf16[640,128]{0,1:T(8,128)(2,1)S(1)}, u32[]{:S(2)}, u32[]{:S(2)}) collective-permute-start(bf16[640,128]{0,1:T(8,128)(2,1)S(1)} %get-tuple-element.10), channel_id=1, source_target_pairs={{0,4},{4,8},{8,12},{12,16},{16,20},{20,24},{24,28},{1,5},{5,9},{9,... | collective-permute-start | bytes 491528 | tf_op jit(solution)/shard_map/ppermute | solution.py:14
  74.5 12.0 %collective-permute-start.13 = (bf16[640,128]{0,1:T(8,128)(2,1)S(1)}, bf16[640,128]{0,1:T(8,128)(2,1)S(1)}, u32[]{:S(2)}, u32[]{:S(2)}) collective-permute-start(bf16[640,128]{0,1:T(8,128)(2,1)S(1)} %get-tuple-element.11), channel_id=1, source_target_pairs={{4,0},{8,4},{12,8},{16,12},{20,16},{24,20},{28,24},{5,1},{9,5},{13... | collective-permute-start | bytes 491528 | tf_op jit(solution)/shard_map/ppermute | solution.py:14
  76.4 6.5 %collective-permute-start.14 = (bf16[384,128]{0,1:T(8,128)(2,1)S(1)}, bf16[384,128]{0,1:T(8,128)(2,1)S(1)}, u32[]{:S(2)}, u32[]{:S(2)}) collective-permute-start(bf16[384,128]{0,1:T(8,128)(2,1)S(1)} %get-tuple-element.12), channel_id=1, source_target_pairs={{0,1},{1,2},{2,3},{4,5},{5,6},{6,7},{8,9},{9,10},{10,11},{12,13},{... | collective-permute-start | bytes 294920 | tf_op jit(solution)/shard_map/ppermute | solution.py:14
  80.5 6.0 %collective-permute-start.15 = (bf16[384,128]{0,1:T(8,128)(2,1)S(1)}, bf16[384,128]{0,1:T(8,128)(2,1)S(1)}, u32[]{:S(2)}, u32[]{:S(2)}) collective-permute-start(bf16[384,128]{0,1:T(8,128)(2,1)S(1)} %get-tuple-element.13), channel_id=1, source_target_pairs={{1,0},{2,1},{3,2},{5,4},{6,5},{7,6},{9,8},{10,9},{11,10},{13,12},{... | collective-permute-start | bytes 294920 | tf_op jit(solution)/shard_map/ppermute | solution.py:14
where the time goes:
time: 88.7 us; the launch traced here: 87.6 us
  starting transfers between devices  46.7 us (53%)
  matrix products  26.7 us (30%)
  local copies, waits for them, and re-layouts  4.94 us (6%)
  between operations  3.65 us (4%)
  waiting for transfers between devices  3.58 us (4%)
  other arithmetic  2.01 us (2%)
    ppermute x16, starting transfers between devices, shifted(): lax.ppermute(value, axis, [(source, source + steps) for source in range(l...  46.7 us
    dot_general x12, matrix products, apply_operator(): jnp.dot(oper[0, :, start:stop], piece, preferred_element_type=jnp.float32)  14.2 us
    dot_general x12, matrix products, apply_operator(): jnp.dot(oper[1, :, start:stop], piece, preferred_element_type=jnp.float32)  12.5 us
    ppermute x16, waiting for transfers between devices, shifted(): lax.ppermute(value, axis, [(source, source + steps) for source in range(l...  3.58 us
    unnamed x5, local copies, waits for them, and re-layouts  3.25 us
  transfers between devices with their start and end apart: 16, of which 1 were waited for; matrix products, arithmetic and copies ran while one was open for 25% of the time, Pallas kernels for 0%

commit v1 on v0

v1 whole, which is shorter than its diff:
```python
import functools

import jax
import jax.numpy as jnp
from jax import lax
from jax.experimental import pallas as pl
from jax.experimental.pallas import tpu as pltpu
from jax.sharding import PartitionSpec as P

FACE_LONG = 640
FACE_SHORT = 384
ITERS = 3
TILE = 512
MESH = pl.DeviceIdType.MESH


def kernel(n_wide, n_narrow, oper_hbm, src_hbm, len_ref, out_hbm, inc_hbm,
           w, src, xs, x2, acc, outs, zeros,
           w_sem, ws_sem, src_sem, send_sem, recv_sem, fin_sem, zero_sem):
    total = src.shape[0]
    short0 = 2 * FACE_LONG
    row = lax.axis_index("wide")
    col = lax.axis_index("narrow")
    far = lax.rem(row, 2)
    near = 1 - far
    first = jnp.where(2 * col < n_narrow, 1, 0)
    second = 1 - first

    def long_off(face):
        return pl.multiple_of(face * FACE_LONG, 128)

    def short_off(face):
        return pl.multiple_of(short0 + face * FACE_SHORT, 128)

    def geometry(is_long, face):
        if is_long:
            target = row + 2 * face - 1
            return (long_off(face), long_off(1 - face), FACE_LONG, {"wide": target},
                    (target >= 0) & (target < n_wide), face)
        target = col + 2 * face - 1
        return (short_off(face), short_off(1 - face), FACE_SHORT, {"narrow": target},
                (target >= 0) & (target < n_narrow), 2 + face)

    faces = [(False, first), (False, second), (True, far), (True, near)]

    def send(step, is_long, face, start):
        here, there, size, device, exists, slot = geometry(is_long, face)
        other = (2 + 1 - face) if is_long is False else 1 - face
        source = src if step == 0 else outs.at[step - 1]
        target = inc_hbm if step == ITERS else xs.at[step]
        copy = pltpu.make_async_remote_copy(
            src_ref=source.at[pl.ds(here, size)],
            dst_ref=target.at[pl.ds(there, size)],
            send_sem=send_sem.at[step, slot],
            recv_sem=recv_sem.at[step, other],
            device_id=device,
            device_id_type=MESH,
        )

        @pl.when(exists)
        def _():
            if start:
                copy.start()
            else:
                copy.wait_send()

    def receive(step, is_long, face):
        here, there, size, device, exists, slot = geometry(is_long, face)
        source = src if step == 0 else outs.at[step - 1]
        target = inc_hbm if step == ITERS else xs.at[step]
        copy = pltpu.make_async_remote_copy(
            src_ref=source.at[pl.ds(here, size)],
            dst_ref=target.at[pl.ds(here, size)],
            send_sem=send_sem.at[step, slot],
            recv_sem=recv_sem.at[step, slot],
            device_id=device,
            device_id_type=MESH,
        )

        @pl.when(exists)
        def _():
            copy.wait_recv()

    src_copy = pltpu.make_async_copy(src_hbm.at[0, 0], src, src_sem)
    src_copy.start()

    barrier = pltpu.get_barrier_semaphore()
    count = jnp.int32(0)
    for is_long, face in faces:
        _, _, _, device, exists, _ = geometry(is_long, face)
        count = count + exists.astype(jnp.int32)

        @pl.when(exists)
        def _():
            pl.semaphore_signal(barrier, inc=1, device_id=device, device_id_type=MESH)

    def load_long(which, face, tile):
        rows = pl.ds(pl.multiple_of(tile * TILE, TILE), TILE)
        cols = pl.ds(long_off(face), FACE_LONG)
        return pltpu.make_async_copy(
            oper_hbm.at[0, 0, :, rows, cols], w.at[:, rows, cols], w_sem.at[which, tile])

    def load_short():
        cols = pl.ds(short0, 2 * FACE_SHORT)
        return pltpu.make_async_copy(
            oper_hbm.at[0, 0, :, :, cols], w.at[:, :, cols], ws_sem)

    tiles = total // TILE
    for tile in range(tiles):
        load_long(0, near, tile).start()

    pl.semaphore_wait(barrier, count)
    src_copy.wait()
    for is_long, face in faces:
        send(0, is_long, face, True)

    for tile in range(tiles):
        load_long(1, far, tile).start()
    load_short().start()

    zeros[...] = jnp.zeros_like(zeros)
    for is_long, face in faces:
        here, _, size, _, exists, slot = geometry(is_long, face)

        @pl.when(jnp.logical_not(exists))
        def _():
            for step in range(ITERS):
                xs[step, pl.ds(here, size), :] = jnp.zeros((size, xs.shape[2]), xs.dtype)
            pltpu.make_async_copy(
                zeros.at[pl.ds(0, size)], inc_hbm.at[pl.ds(here, size)], zero_sem.at[slot]).start()

    def live(slot, size):
        return lax.broadcasted_iota(jnp.int32, (size, xs.shape[2]), 0) < len_ref[0, 0, slot]

    half = xs.shape[2] // 2

    def prepare(step, here, size, slot):
        value = xs[step, pl.ds(here, size), :].astype(jnp.float32)
        if step == 0:
            value = jnp.where(live(slot, size), value, 0.0)
            xs[step, pl.ds(here, size), :] = value.astype(xs.dtype)
        lanes = lax.broadcasted_iota(jnp.int32, value.shape, 1)
        turned = pltpu.roll(value, half, 1)
        x2[pl.ds(here, size), :] = jnp.where(lanes < half, -turned, turned).astype(x2.dtype)

    def product(step, rows, cols):
        return (jnp.dot(w[0, rows, cols], xs[step, cols, :], preferred_element_type=jnp.float32)
                + jnp.dot(w[1, rows, cols], x2[cols, :], preferred_element_type=jnp.float32))

    for step in range(ITERS):
        for which, face in ((0, near), (1, far)):
            receive(step, True, face)
            here = long_off(face)
            prepare(step, here, FACE_LONG, face)
            cols = pl.ds(here, FACE_LONG)

            @pl.loop(0, tiles)
            def _(tile):
                rows = pl.ds(pl.multiple_of(tile * TILE, TILE), TILE)
                if step == 0:
                    load_long(which, face, tile).wait()
                base = src[rows, :].astype(jnp.float32) if which == 0 else acc[rows, :]
                acc[rows, :] = base + product(step, rows, cols)

        if step == 0:
            load_short().wait()
        for face in (0, 1):
            receive(step, False, face)
            prepare(step, short0 + face * FACE_SHORT, FACE_SHORT, 2 + face)
        cols = pl.ds(short0, 2 * FACE_SHORT)
        for is_long, face in faces:
            here, _, size, _, _, slot = geometry(is_long, face)
            rows = pl.ds(here, size)
            value = acc[rows, :] + product(step, rows, cols)
            outs[step, rows, :] = jnp.where(live(slot, size), value, 0.0).astype(outs.dtype)
            send(step + 1, is_long, face, True)

    final = pltpu.make_async_copy(outs.at[ITERS - 1], out_hbm, fin_sem)
    final.start()
    for step in range(ITERS + 1):
        for is_long, face in faces:
            send(step, is_long, face, False)
    for is_long, face in faces:
        here, _, size, _, exists, slot = geometry(is_long, face)
        receive(ITERS, is_long, face)

        @pl.when(jnp.logical_not(exists))
        def _():
            pltpu.make_async_copy(
                zeros.at[pl.ds(0, size)], inc_hbm.at[pl.ds(here, size)], zero_sem.at[slot]).wait()
    final.wait()


def body(n_wide, n_narrow, operator, sources, face_lengths):
    total, width = sources.shape[2:]
    dtype = sources.dtype
    shape = jax.ShapeDtypeStruct((total, width), dtype)
    outgoing, incoming = pl.pallas_call(
        functools.partial(kernel, n_wide, n_narrow),
        out_shape=(shape, shape),
        in_specs=[
            pl.BlockSpec(memory_space=pl.ANY),
            pl.BlockSpec(memory_space=pl.ANY),
            pl.BlockSpec(memory_space=pltpu.SMEM),
        ],
        out_specs=[pl.BlockSpec(memory_space=pl.ANY)] * 2,
        scratch_shapes=[
            pltpu.VMEM((2, total, total), dtype),
            pltpu.VMEM((total, width), dtype),
            pltpu.VMEM((ITERS, total, width), dtype),
            pltpu.VMEM((total, width), dtype),
            pltpu.VMEM((total, width), jnp.float32),
            pltpu.VMEM((ITERS, total, width), dtype),
            pltpu.VMEM((FACE_LONG, width), dtype),
            pltpu.SemaphoreType.DMA((2, total // TILE)),
            pltpu.SemaphoreType.DMA,
            pltpu.SemaphoreType.DMA,
            pltpu.SemaphoreType.DMA((ITERS + 1, 4)),
            pltpu.SemaphoreType.DMA((ITERS + 1, 4)),
            pltpu.SemaphoreType.DMA,
            pltpu.SemaphoreType.DMA((4,)),
        ],
        compiler_params=pltpu.CompilerParams(collective_id=0, has_side_effects=True),
        name="schwarz",
    )(operator, sources, face_lengths)
    return outgoing[None, None], incoming[None, None]


def solution(mesh):
    in_specs = (
        P("wide", "narrow", None, None, None),
        P("wide", "narrow", None, None),
        P("wide", "narrow", None),
    )
    out_specs = (P("wide", "narrow", None, None), P("wide", "narrow", None, None))
    step = functools.partial(body, mesh.shape["wide"], mesh.shape["narrow"])
    return jax.shard_map(step, mesh=mesh, in_specs=in_specs, out_specs=out_specs, check_vma=False)
```

time: 88.7 us -> 37.6 us (0.42)
  starting transfers between devices: 46.7 us -> 0 us
  Pallas kernels: 0 us -> 33 us
  matrix products: 26.7 us -> 0 us
  waiting for transfers between devices: 3.58 us -> 0 us
  between operations: 3.65 us -> 0.64 us
  other arithmetic: 2.01 us -> 0 us
  local copies, waits for them, and re-layouts: 4.94 us -> 3.74 us
    ppermute x16 -> x0, starting transfers between devices: 46.7 us -> none  [shifted(): lax.ppermute(value, axis, [(source, source + steps) for source in range(l...]
    pallas_call x0 -> x1, Pallas kernels: none -> 33 us  [body(): pl.pallas_call(functools.partial(kernel, n_wide, n_narrow), out_shape=(sh...]
    dot_general x24 -> x0, matrix products: 26.7 us -> none  [the longest x12 14.2 us: apply_operator(): jnp.dot(oper[0, :, start:stop], piece, preferred_element_type=jnp.float32)]
    ppermute x16 -> x0, waiting for transfers between devices: 3.58 us -> none  [shifted(): lax.ppermute(value, axis, [(source, source + steps) for source in range(l...]
    slice x9 -> x0, local copies, waits for them, and re-layouts: 1.68 us -> none  [the longest x1 1.47 us: live_rows(): live = live | (rows >= edges[face]) & (rows < edges[face] + counts[face])]
    or x1 -> x0, other arithmetic: 0.94 us -> none  [live_rows(): live = live | (rows >= edges[face]) & (rows < edges[face] + counts[face])]
    unnamed x5 -> x2, local copies, waits for them, and re-layouts: 3.25 us -> 3.74 us
  transfers between devices with their start and end apart: 16 -> 0, of which waited for: 1 -> 0; matrix products, arithmetic and copies ran while one was open for 25% -> 0% of each run, Pallas kernels for 0% -> 0%
where the time goes in v1:
time: 37.6 us; the launch traced here: 37.3 us
  Pallas kernels  33 us (88%)
  local copies, waits for them, and re-layouts  3.74 us (10%)
  between operations  0.64 us (2%)
    pallas_call x1, Pallas kernels, body(): pl.pallas_call(functools.partial(kernel, n_wide, n_narrow), out_shape=(sh...  33 us
    unnamed x2, local copies, waits for them, and re-layouts  3.74 us

profile of v1, /device:TPU:1, one launch (start us, length us, event | category | flops | bytes accessed | tf_op | source)
XLA Modules:
  0.0 37.3 jit_solution(13176326278911460664)
XLA Ops:
  0.6 33.0 %schwarz.1 = (bf16[2048,128]{1,0:T(8,128)(2,1)}, bf16[2048,128]{1,0:T(8,128)(2,1)}) custom-call(bf16[1,1,2,2048,2048]{4,3,2,1,0:T(8,128)(2,1)} %oper_hbm.1, bf16[1,1,2048,128]{3,2,1,0:T(8,128)(2,1)} %src_hbm.1, s32[1,1,4]{2,1,0:T(1,128)} %len_ref.1), custom_call_target="tpu_custom_call" | custom-call | tf_op jit(solution)/shard_map/schwarz/pallas_call | solution.py:198
  33.6 1.9 %copy.7 = bf16[1,1,2048,128]{3,2,1,0:T(8,128)(2,1)} copy(bf16[1,1,2048,128]{3,2,1,0:T(8,128)(2,1)} %bitcast.3) | data formatting | bytes 1048576
  35.5 1.9 %copy.8 = bf16[1,1,2048,128]{3,2,1,0:T(8,128)(2,1)} copy(bf16[1,1,2048,128]{3,2,1,0:T(8,128)(2,1)} %bitcast.2) | data formatting | bytes 1048576

commit v2 on v1

v2 whole, which is shorter than its diff:
```python
import functools

import jax
import jax.numpy as jnp
from jax import lax
from jax.experimental import pallas as pl
from jax.experimental.pallas import tpu as pltpu
from jax.sharding import PartitionSpec as P

FACE_LONG = 640
FACE_SHORT = 384
ITERS = 3
TILE = 1024
MESH = pl.DeviceIdType.MESH


def kernel(n_wide, n_narrow, oper_hbm, src_hbm, len_ref, last_out, last_in,
           w, src, xs, acc, outs,
           w_sem, src_sem, send_sem, recv_sem):
    total = src.shape[0]
    short0 = 2 * FACE_LONG
    row = lax.axis_index("wide")
    col = lax.axis_index("narrow")
    far = lax.rem(row, 2)
    near = 1 - far
    first = jnp.where(2 * col < n_narrow, 1, 0)
    second = 1 - first

    def long_off(face):
        return pl.multiple_of(face * FACE_LONG, 128)

    def short_off(face):
        return pl.multiple_of(short0 + face * FACE_SHORT, 128)

    def geometry(is_long, face):
        if is_long:
            target = row + 2 * face - 1
            return (long_off(face), long_off(1 - face), FACE_LONG, {"wide": target},
                    (target >= 0) & (target < n_wide), face)
        target = col + 2 * face - 1
        return (short_off(face), short_off(1 - face), FACE_SHORT, {"narrow": target},
                (target >= 0) & (target < n_narrow), 2 + face)

    def sent_from(step):
        return src if step == 0 else last_out if step == ITERS else outs.at[step - 1]

    def landed_in(step):
        return last_in if step == ITERS else xs.at[step]

    def landing(step, there):
        return there if step == ITERS else pl.multiple_of(2 * there, 128)

    faces = [(False, first), (False, second), (True, far), (True, near)]

    def send(step, is_long, face, start):
        here, there, size, device, exists, slot = geometry(is_long, face)
        other = (2 + 1 - face) if is_long is False else 1 - face
        source, target = sent_from(step), landed_in(step)
        copy = pltpu.make_async_remote_copy(
            src_ref=source.at[pl.ds(here, size)],
            dst_ref=target.at[pl.ds(landing(step, there), size)],
            send_sem=send_sem.at[step, slot],
            recv_sem=recv_sem.at[step, other],
            device_id=device,
            device_id_type=MESH,
        )

        @pl.when(exists)
        def _():
            if start:
                copy.start()
            else:
                copy.wait_send()

    def receive(step, is_long, face):
        here, there, size, device, exists, slot = geometry(is_long, face)
        source, target = sent_from(step), landed_in(step)
        copy = pltpu.make_async_remote_copy(
            src_ref=source.at[pl.ds(here, size)],
            dst_ref=target.at[pl.ds(landing(step, here), size)],
            send_sem=send_sem.at[step, slot],
            recv_sem=recv_sem.at[step, slot],
            device_id=device,
            device_id_type=MESH,
        )

        @pl.when(exists)
        def _():
            copy.wait_recv()

    src_copy = pltpu.make_async_copy(src_hbm.at[0, 0], src, src_sem)
    src_copy.start()

    barrier = pltpu.get_barrier_semaphore()
    count = jnp.int32(0)
    for is_long, face in faces:
        _, _, _, device, exists, _ = geometry(is_long, face)
        count = count + exists.astype(jnp.int32)

        @pl.when(exists)
        def _():
            pl.semaphore_signal(barrier, inc=1, device_id=device, device_id_type=MESH)

    def loads(is_long, face):
        here, _, size, _, _, slot = geometry(is_long, face)
        return [pltpu.make_async_copy(
            oper_hbm.at[0, 0, part, :, pl.ds(here, size)],
            w.at[:, pl.ds(pl.multiple_of(2 * here + part * size, 128), size)],
            w_sem.at[part, slot]) for part in range(2)]

    def load(is_long, face):
        for copy in loads(is_long, face):
            copy.start()

    def loaded(is_long, face):
        for copy in loads(is_long, face):
            copy.wait()

    load(True, near)

    pl.semaphore_wait(barrier, count)
    src_copy.wait()
    for is_long, face in faces:
        send(0, is_long, face, True)

    load(True, far)
    load(False, 0)
    load(False, 1)

    for is_long, face in faces:
        here, _, size, _, exists, slot = geometry(is_long, face)

        @pl.when(jnp.logical_not(exists))
        def _():
            for step in range(ITERS + 1):
                rows = pl.ds(landing(step, here), size)
                landed_in(step)[rows, :] = jnp.zeros((size, xs.shape[2]), xs.dtype)

    def live(slot, size):
        return lax.broadcasted_iota(jnp.int32, (size, xs.shape[2]), 0) < len_ref[0, 0, slot]

    half = xs.shape[2] // 2

    def prepare(step, is_long, face):
        here, _, size, _, _, slot = geometry(is_long, face)
        rows = pl.ds(landing(step, here), size)
        value = xs[step, rows, :].astype(jnp.float32)
        if step == 0:
            value = jnp.where(live(slot, size), value, 0.0)
            xs[step, rows, :] = value.astype(xs.dtype)
        lanes = lax.broadcasted_iota(jnp.int32, value.shape, 1)
        turned = pltpu.roll(value, half, 1)
        rows = pl.ds(pl.multiple_of(2 * here + size, 128), size)
        xs[step, rows, :] = jnp.where(lanes < half, -turned, turned).astype(xs.dtype)

    def product(step, rows, cols):
        return jnp.dot(w[rows, cols], xs[step, cols, :], preferred_element_type=jnp.float32)

    for step in range(ITERS):
        for which, face in ((0, near), (1, far)):
            if step == 0:
                loaded(True, face)
            receive(step, True, face)
            prepare(step, True, face)
            cols = pl.ds(pl.multiple_of(2 * long_off(face), 128), 2 * FACE_LONG)

            @pl.loop(0, total // TILE)
            def _(tile):
                rows = pl.ds(pl.multiple_of(tile * TILE, TILE), TILE)
                base = src[rows, :].astype(jnp.float32) if which == 0 else acc[rows, :]
                acc[rows, :] = base + product(step, rows, cols)

        for face in (0, 1):
            if step == 0:
                loaded(False, face)
        for face in (0, 1):
            receive(step, False, face)
            prepare(step, False, face)
        cols = pl.ds(2 * short0, 4 * FACE_SHORT)
        for is_long, face in faces:
            here, _, size, _, _, slot = geometry(is_long, face)
            rows = pl.ds(here, size)
            value = acc[rows, :] + product(step, rows, cols)
            sent_from(step + 1)[rows, :] = jnp.where(live(slot, size), value, 0.0).astype(xs.dtype)
            send(step + 1, is_long, face, True)

    for step in range(ITERS + 1):
        for is_long, face in faces:
            send(step, is_long, face, False)
    for is_long, face in faces:
        receive(ITERS, is_long, face)


def write_out(out_ref, in_ref, out_hbm, in_hbm, sem):
    copies = [pltpu.make_async_copy(out_ref, out_hbm.at[0, 0], sem.at[0]),
              pltpu.make_async_copy(in_ref, in_hbm.at[0, 0], sem.at[1])]
    for copy in copies:
        copy.start()
    for copy in copies:
        copy.wait()


def body(n_wide, n_narrow, operator, sources, face_lengths):
    total, width = sources.shape[2:]
    dtype = sources.dtype
    held = pltpu.VMEM((total, width), dtype)
    outgoing, incoming = pl.pallas_call(
        functools.partial(kernel, n_wide, n_narrow),
        out_shape=(held, held),
        in_specs=[
            pl.BlockSpec(memory_space=pltpu.HBM),
            pl.BlockSpec(memory_space=pltpu.HBM),
            pl.BlockSpec(memory_space=pltpu.SMEM),
        ],
        out_specs=[pl.BlockSpec(memory_space=pltpu.VMEM)] * 2,
        scratch_shapes=[
            pltpu.VMEM((total, 2 * total), dtype),
            pltpu.VMEM((total, width), dtype),
            pltpu.VMEM((ITERS, 2 * total, width), dtype),
            pltpu.VMEM((total, width), jnp.float32),
            pltpu.VMEM((ITERS - 1, total, width), dtype),
            pltpu.SemaphoreType.DMA((2, 4)),
            pltpu.SemaphoreType.DMA,
            pltpu.SemaphoreType.DMA((ITERS + 1, 4)),
            pltpu.SemaphoreType.DMA((ITERS + 1, 4)),
        ],
        compiler_params=pltpu.CompilerParams(
            collective_id=0, has_side_effects=True, vmem_limit_bytes=54 * 1024 * 1024),
        name="schwarz",
    )(operator, sources, face_lengths)
    shape = jax.ShapeDtypeStruct(sources.shape, dtype)
    return pl.pallas_call(
        write_out,
        out_shape=(shape, shape),
        in_specs=[pl.BlockSpec(memory_space=pltpu.VMEM)] * 2,
        out_specs=[pl.BlockSpec(memory_space=pl.ANY)] * 2,
        scratch_shapes=[pltpu.SemaphoreType.DMA((2,))],
        compiler_params=pltpu.CompilerParams(vmem_limit_bytes=4 * 1024 * 1024),
        name="write_out",
    )(outgoing, incoming)


def solution(mesh):
    in_specs = (
        P("wide", "narrow", None, None, None),
        P("wide", "narrow", None, None),
        P("wide", "narrow", None),
    )
    out_specs = (P("wide", "narrow", None, None), P("wide", "narrow", None, None))
    step = functools.partial(body, mesh.shape["wide"], mesh.shape["narrow"])
    return jax.shard_map(step, mesh=mesh, in_specs=in_specs, out_specs=out_specs, check_vma=False)
```

time: 37.6 us -> 33.7 us (0.90)
  local copies, waits for them, and re-layouts: 3.74 us -> 0 us
    unnamed x2 -> x0, local copies, waits for them, and re-layouts: 3.74 us -> none
    pallas_call x1 -> x2, Pallas kernels: 33 us -> 32.9 us  [the longest x1 31.9 us: body(): pl.pallas_call(functools.partial(kernel, n_wide, n_narrow), out_shape=(he...]
where the time goes in v2:
time: 33.7 us; the launch traced here: 33.5 us
  Pallas kernels  32.9 us (98%)
  between operations  0.64 us (2%)
    pallas_call x1, Pallas kernels, body(): pl.pallas_call(functools.partial(kernel, n_wide, n_narrow), out_shape=(he...  31.9 us
    pallas_call x1, Pallas kernels, body(): pl.pallas_call(write_out, out_shape=(shape, shape), in_specs=[pl.BlockSpe...  0.99 us

profile of v2, /device:TPU:1, one launch (start us, length us, event | category | flops | bytes accessed | tf_op | source)
XLA Modules:
  0.0 33.5 jit_solution(9189421350814201587)
XLA Ops:
  0.6 31.9 %schwarz.1 = (bf16[2048,128]{1,0:T(8,128)(2,1)S(1)}, bf16[2048,128]{1,0:T(8,128)(2,1)S(1)}) custom-call(bf16[1,1,2,2048,2048]{4,3,2,1,0:T(8,128)(2,1)} %oper_hbm.1, bf16[1,1,2048,128]{3,2,1,0:T(8,128)(2,1)} %src_hbm.1, s32[1,1,4]{2,1,0:T(1,128)} %len_ref.1), custom_call_target="tpu_custom_call" | custom-call | tf_op jit(solution)/shard_map/schwarz/pallas_call | solution.py:207
  32.5 1.0 %write_out.1 = (bf16[1,1,2048,128]{3,2,1,0:T(8,128)(2,1)}, bf16[1,1,2048,128]{3,2,1,0:T(8,128)(2,1)}) custom-call(bf16[2048,128]{1,0:T(8,128)(2,1)S(1)} %get-tuple-element.4.out_ref, bf16[2048,128]{1,0:T(8,128)(2,1)S(1)} %get-tuple-element.5.in_ref), custom_call_target="tpu_custom_call" | custom-call | tf_op jit(solution)/shard_map/write_out/pallas_call | solution.py:232
